TPU v7x, 512 devices: a whole 4x8x8 slice. The times are simulated.
512 devices in a mesh: dp: 8 (over y_hi, x), expert: 64 (over z, y_lo, core).
Axes of the slice: x: 4, y: 8 (y_hi: 2, y_lo: 4; y = y_hi * 4 + y_lo), z: 8, core: 2. Of those that a mesh axis runs over, the one named last changes fastest.
Arguments:
- tokens: bfloat16 [65536, 1024], P(('dp', 'expert')), may hold values from -6 to 6
- out_grad: bfloat16 [65536, 1024], P(('dp', 'expert')), may hold values from -6 to 6
- expert_ids: int32 [65536, 3], P(('dp', 'expert')), may hold values from 0 to 63, all different within a row; in each aligned block of 128 rows (0 to 127, 128 to 255, ...) at most 7 rows name the same one
- gate_probs: float32 [65536, 3], P(('dp', 'expert')), may hold values from 0.1 to 0.6
- saved_pre: bfloat16 [8, 64, 448, 1536], P('dp', 'expert'), may hold values from -6 to 6
- gate_weight: bfloat16 [64, 1024, 768], P('expert', 'dp'), may hold values from -0.1875 to 0.1875
- up_weight: bfloat16 [64, 1024, 768], P('expert', 'dp'), may hold values from -0.1875 to 0.1875
- down_weight: bfloat16 [64, 1024, 768], P('expert', 'dp'), may hold values from -0.21875 to 0.21875
- basis: bfloat16 [64, 1024, 256], P('expert', 'dp'), may hold values from -0.1875 to 0.1875
Outputs:
- in_grad: bfloat16 [65536, 1024], P(('dp', 'expert'))
- proj_grads: float32 [64, 3, 256, 768], P('expert', None, 'dp')
Inputs may be any that keep to these rules, and one draw needn't show every extreme that they name: `expert_ids`: each token names 3 different experts. The rows of one device name one expert at most 7 times, and on some devices some expert exactly 7 times.
All inputs are finite; a program needn't handle non-finite values.
Results may differ from a plain program's by a relative error of at most 0.0091.
Values may be sent and summed in bfloat16 or wider, within the bound.
A program may use at most 64 MiB of HBM per device.

v0:
```python
import jax
import jax.numpy as jnp
from jax import lax
from jax.sharding import Mesh
from jax.sharding import PartitionSpec as P

DP = ("dp_0", "dp_1")
DP_EXPERT = ("dp_0", "dp_1", "expert")


def side_by_side(arrays, axis, split_dim, concat_dim, along):
    widths = [a.shape[along] for a in arrays]
    both = jnp.concatenate(arrays, axis=along)
    filled = lax.all_to_all(both, axis, split_axis=split_dim, concat_axis=concat_dim, tiled=True)
    return tuple(jnp.split(filled, [sum(widths[:k]) for k in range(1, len(widths))], axis=along))


def side_by_side_2(arrays, axis, dim, along):
    both = jnp.concatenate(arrays, axis=along)
    filled, at, outs = (lax.all_gather(both, axis, axis=dim, tiled=True), 0, [])
    for a in arrays:
        outs.append(lax.slice_in_dim(filled, at, at + a.shape[along], axis=along))
        at += a.shape[along]
    return tuple(outs)


def sum_in_order(tiles, axes, sequence):
    dims = [lax.axis_size(a) for a in axes]
    tiles = tiles.reshape(*dims, *tiles.shape[1:])
    tiles = tiles.transpose(*sequence, *range(len(axes), tiles.ndim))
    tiles = tiles.reshape(-1, *tiles.shape[len(axes) :])
    for k in sequence:
        tiles = lax.psum_scatter(tiles, axes[k], scatter_dimension=0, tiled=True)
    return tiles[0]


def cut_along(value, dim, peers):
    dims = value.shape
    tiles = value.reshape(*dims[:dim], peers, dims[dim] // peers, *dims[dim + 1 :])
    return jnp.moveaxis(tiles, dim, 0)


def scatter_axes(value, axes, sequence, dim):
    peers = lax.axis_size(axes)
    return sum_in_order(cut_along(value, dim, peers), axes, sequence)


def contract_rows(left, right):
    return lax.dot_general(
        left, right, (((0,), (0,)), ((), ())), preferred_element_type=jnp.float32
    )


def contract_cols(left, right):
    return lax.dot_general(
        left, right, (((1,), (1,)), ((), ())), preferred_element_type=jnp.float32
    )


def body(
    tokens, out_grad, expert_ids, gate_probs, saved_pre, gate_weight, up_weight, down_weight, basis
):
    n_owner = lax.axis_size("expert")
    tok_rows, width = tokens.shape
    topk = expert_ids.shape[1]
    slots = saved_pre.shape[2]
    cap = slots // n_owner
    hidden = gate_weight.shape[2]
    onehot = (expert_ids[:, :, None] == jnp.arange(n_owner, dtype=jnp.int32)[None, None, :]).astype(
        jnp.int32
    )
    per_token = jnp.sum(onehot, axis=1)
    before = jnp.cumsum(per_token, axis=0) - per_token
    position = jnp.sum(onehot * before[:, None, :], axis=2)
    target = expert_ids * cap + position
    token_index = jnp.broadcast_to(jnp.arange(tok_rows, dtype=jnp.int32)[:, None], target.shape)
    choice_index = jnp.broadcast_to(jnp.arange(topk, dtype=jnp.int32)[None, :], target.shape)
    fill_token = (
        jnp.full((n_owner * cap,), -1, jnp.int32)
        .at[target.reshape(-1)]
        .set(token_index.reshape(-1))
    )
    fill_choice = (
        jnp.zeros((n_owner * cap,), jnp.int32).at[target.reshape(-1)].set(choice_index.reshape(-1))
    )
    filled = fill_token >= 0
    picked = jnp.maximum(fill_token, 0)
    send_rows = jnp.where(filled[:, None], tokens[picked], jnp.zeros((), jnp.bfloat16))
    weight_pick = gate_probs[picked, fill_choice]
    scaled = (out_grad[picked].astype(jnp.float32) * weight_pick[:, None]).astype(jnp.bfloat16)
    send_grad = jnp.where(filled[:, None], scaled, jnp.zeros((), jnp.bfloat16))
    arrived_rows, arrived_grad = side_by_side(
        (send_rows.reshape(n_owner, cap, width), send_grad.reshape(n_owner, cap, width)),
        "expert",
        0,
        0,
        1,
    )
    rows_in = arrived_rows.reshape(slots, width)
    grad_in = arrived_grad.reshape(slots, width)
    full_down, full_basis, full_gate, full_up = side_by_side_2(
        (down_weight, basis, gate_weight, up_weight), DP, 1, 2
    )
    pieces = (full_down, full_basis)
    down_piece = pieces[0][0]
    basis_piece = pieces[1][0]
    hidden_grad = jnp.dot(grad_in, down_piece, preferred_element_type=jnp.float32)
    x_acc = jnp.dot(rows_in, basis_piece, preferred_element_type=jnp.float32)
    dy_acc = jnp.dot(grad_in, basis_piece, preferred_element_type=jnp.float32)
    hidden_grad, x_acc, dy_acc = (hidden_grad, x_acc, dy_acc)
    pre = saved_pre[0, 0].astype(jnp.float32)
    gate_pre = pre[:, :hidden]
    up_pre = pre[:, hidden:]
    sig = jax.nn.sigmoid(gate_pre)
    hid = (gate_pre * sig * up_pre).astype(jnp.bfloat16)
    up_grad = (hidden_grad * gate_pre * sig).astype(jnp.bfloat16)
    gate_grad = (hidden_grad * up_pre * sig * (1.0 + gate_pre * (1.0 - sig))).astype(jnp.bfloat16)
    x_proj = x_acc.astype(jnp.bfloat16)
    dy_proj = dy_acc.astype(jnp.bfloat16)
    pieces = (full_gate, full_up)
    row_grad = contract_cols(gate_grad, pieces[0][0]) + contract_cols(up_grad, pieces[1][0])
    terms = jnp.stack(
        [
            contract_rows(x_proj, gate_grad),
            contract_rows(x_proj, up_grad),
            contract_rows(dy_proj, hid),
        ]
    )
    proj_grads = scatter_axes(terms[None].astype(jnp.bfloat16), DP, (1, 0), 2).astype(jnp.float32)
    returned = lax.all_to_all(
        row_grad.astype(jnp.bfloat16).reshape(n_owner, cap, width),
        "expert",
        split_axis=0,
        concat_axis=0,
        tiled=True,
    )
    returned = returned.reshape(n_owner * cap, width)
    in_grad = jnp.sum(returned[target].astype(jnp.float32), axis=1).astype(jnp.bfloat16)
    return (in_grad, proj_grads)


def solution(mesh):
    finer = Mesh(mesh.devices.reshape(2, 4, mesh.shape["expert"]), ("dp_0", "dp_1", "expert"))
    placed = (
        P(DP_EXPERT, None),
        P(DP_EXPERT, None),
        P(DP_EXPERT, None),
        P(DP_EXPERT, None),
        P(DP, "expert", None, None),
        P("expert", DP, None),
        P("expert", DP, None),
        P("expert", DP, None),
        P("expert", DP, None),
    )
    return jax.shard_map(
        body,
        mesh=finer,
        in_specs=placed,
        out_specs=(P(DP_EXPERT, None), P("expert", None, DP, None)),
        check_vma=False,
    )
```

profile of v0, /device:TPU:9, one launch (start us, length us, event | category | flops | bytes accessed | tf_op | source)
XLA Modules:
  0.0 236.9 jit_solution(16643770522436022008)
XLA Ops:
  7.2 2.1 pad_maximum_fusion.2
  10.6 2.9 %scatter_custom_fusion.1 = s32[448]{0:T(512)S(1)} fusion(s32[384]{0:T(512)S(1)} %fusion.7, s32[384]{0:T(512)S(1)} %reshape.218, s32[]{:T(128)} %constant.9.clone.1), kind=kCustom, calls=%fused_computation.44 | custom fusion | bytes 1796 | tf_op jit(solution)/shard_map/scatter | solution.py:84
  13.5 2.9 %scatter_custom_fusion = s32[448]{0:T(512)S(1)} fusion(s32[384]{0:T(512)S(1)} %fusion.7, s32[384]{0:T(512)S(1)} %reshape.210, s32[]{:T(128)} %constant.7.clone.1), kind=kCustom, calls=%fused_computation.48 | custom fusion | bytes 1796 | tf_op jit(solution)/shard_map/scatter | solution.py:81
  16.6 4.0 %gather_fusion.2 = f32[448]{0:T(512)S(1)} fusion(f32[128,3]{0,1:T(4,128)S(1)} %copy-done.1, s32[448]{0:T(512)S(1)} %get-tuple-element.10), kind=kCustom, calls=%fused_computation.2 | custom fusion | bytes 7168 | tf_op jit(solution)/shard_map/gather | solution.py:89
  20.8 2.7 %gather_fusion.1 = bf16[448,1024]{1,0:T(8,128)(2,1)} fusion(bf16[128,1024]{1,0:T(8,128)(2,1)S(1)} %copy-done, s32[1024]{0:T(1024)S(1)} %pad_clamp_fusion.1), kind=kCustom, calls=%fused_computation.1 | custom fusion | bytes 1836800 | tf_op jit(solution)/shard_map/gather | solution.py:90
  23.5 2.1 gather_fusion
  27.6 2.2 pad_maximum_fusion
  29.8 14.7 %all-to-all-start = ((bf16[64,14,1024]{2,1,0:T(8,128)(2,1)}), bf16[64,14,1024]{2,1,0:T(8,128)(2,1)S(1)}, u32[]{:S(2)}, u32[]{:S(2)}) async-start(bf16[64,14,1024]{2,1,0:T(8,128)(2,1)} %pad_maximum_fusion), calls=%async_computation | async-start | bytes 4194304 | tf_op jit(solution)/shard_map/all_to_all | solution.py:14
  44.7 3.2 %bitcast_convert_fusion = f32[448,1536]{1,0:T(8,128)} fusion(bf16[1,1,448,1536]{3,2,1,0:T(8,128)(2,1)} %param.13), kind=kLoop, calls=%fused_computation.15 | loop fusion | flops 688128 | bytes 4128768 | tf_op jit(solution)/shard_map/convert_element_type | solution.py:111
  47.9 107.0 %all-to-all-done = bf16[64,14,1024]{2,1,0:T(8,128)(2,1)S(1)} async-done(((bf16[64,14,1024]{2,1,0:T(8,128)(2,1)}), bf16[64,14,1024]{2,1,0:T(8,128)(2,1)S(1)}, u32[]{:S(2)}, u32[]{:S(2)}) %all-to-all-start) | async-done | bytes 1835040 | tf_op jit(solution)/shard_map/all_to_all | solution.py:14
  154.9 1.6 fusion.13
  156.5 1.4 reshape.170
  159.3 1.5 convolution_convert_fusion.4
  160.9 3.5 %multiply_convert_fusion.3 = (bf16[448,768]{1,0:T(8,128)(2,1)S(1)}, bf16[448,768]{1,0:T(8,128)(2,1)S(1)}) fusion(f32[448,1536]{1,0:T(8,128)} %bitcast_convert_fusion, bf16[448,1024]{1,0:T(8,128)(2,1)S(1)} %copy-done.4, bf16[1,1024,2560]{2,1,0:T(8,128)(2,1)} %all-gather.2.cloned.1.call-done), kind=kOutput, calls=%fused_computation.18 | convolution fusion | flops 709115904 | bytes 6619136 | tf_op jit(solution)/shard_map/dot_general | solution.py:107
  166.9 3.2 %convolution_convert_fusion = bf16[256,768]{1,0:T(8,128)(2,1)} fusion(bf16[448,1024]{1,0:T(8,128)(2,1)} %reshape.167, f32[448,1536]{1,0:T(8,128)S(1)} %copy-done.3, bf16[1,1024,2560]{2,1,0:T(8,128)(2,1)} %all-gather.2.cloned.1.call-done), kind=kOutput, calls=%fused_computation.20 | convolution fusion | flops 413417472 | bytes 4587520 | tf_op jit(solution)/shard_map/dot_general | solution.py:49
  172.7 2.4 %fusion = f32[448,1024]{1,0:T(8,128)S(1)} fusion(bf16[448,768]{1,0:T(8,128)(2,1)S(1)} %copy-done.8, bf16[1,1024,2560]{2,1,0:T(8,128)(2,1)} %all-gather.2.cloned.1.call-done), kind=kOutput, calls=%fused_computation.10 | convolution fusion | flops 704643072 | bytes 4096000 | tf_op jit(solution)/shard_map/dot_general | solution.py:55
  175.0 2.3 add_convert_fusion
  178.6 6.5 %all-to-all-start.1 = ((bf16[64,7,1024]{2,1,0:T(8,128)(2,1)}), bf16[64,7,1024]{2,1,0:T(8,128)(2,1)S(1)}, u32[]{:S(2)}, u32[]{:S(2)}) async-start(bf16[64,7,1024]{2,1,0:T(8,128)(2,1)} %reshape.168), calls=%async_computation.1 | async-start | bytes 2097152 | tf_op jit(solution)/shard_map/all_to_all | solution.py:130
  185.2 13.1 %reduce-scatter.3.cloned.1.call-done = bf16[2,1,3,32,768]{4,3,2,1,0:T(8,128)(2,1)} async-done(((bf16[8,1,3,32,768]{4,3,2,1,0:T(8,128)(2,1)}), bf16[2,1,3,32,768]{4,3,2,1,0:T(8,128)(2,1)}) %reduce-scatter.3.cloned.1.call-update) | async-done | bytes 294928 | tf_op jit(solution)/shard_map/reduce_scatter | solution.py:33
  198.6 15.8 %all-to-all-done.1 = bf16[64,7,1024]{2,1,0:T(8,128)(2,1)S(1)} async-done(((bf16[64,7,1024]{2,1,0:T(8,128)(2,1)}), bf16[64,7,1024]{2,1,0:T(8,128)(2,1)S(1)}, u32[]{:S(2)}, u32[]{:S(2)}) %all-to-all-start.1) | async-done | bytes 917536 | tf_op jit(solution)/shard_map/all_to_all | solution.py:130
  214.7 2.1 gather_fusion.3
  217.3 2.1 reduce_sum.32
  219.4 9.3 %reduce-scatter.5.cloned.1.call-done = bf16[1,1,3,32,768]{4,3,2,1,0:T(8,128)(2,1)} async-done(((bf16[2,1,3,32,768]{4,3,2,1,0:T(8,128)(2,1)}), bf16[1,1,3,32,768]{4,3,2,1,0:T(8,128)(2,1)}) %reduce-scatter.5.cloned.1.call-update) | async-done | bytes 147472 | tf_op jit(solution)/shard_map/reduce_scatter | solution.py:33
  228.7 1.6 bitcast_convert_fusion.1
  (60 shorter events, 12.5 us)
Async XLA Ops:
  7.2 13.6 %copy-start = (bf16[128,1024]{1,0:T(8,128)(2,1)S(1)}, bf16[128,1024]{1,0:T(8,128)(2,1)}, u32[]{:S(2)}) copy-start(bf16[128,1024]{1,0:T(8,128)(2,1)} %param.10) | copy-start | bytes 786436
  7.2 2.2 copy-start.9
  7.2 9.4 %copy-start.1 = (f32[128,3]{0,1:T(4,128)S(1)}, f32[128,3]{0,1:T(4,128)}, u32[]{:S(2)}) copy-start(f32[128,3]{0,1:T(4,128)} %param.12) | copy-start | bytes 4612
  7.2 152.1 %all-gather.2.cloned.1.call-start = ((), (), s32[]{:S(2)}) async-start(), calls=%async_computation.4 | async-start | bytes 5898240 | tf_op jit(solution)/shard_map/all_gather | solution.py:20
  20.8 2.7 %copy-start.2 = (bf16[128,1024]{1,0:T(8,128)(2,1)S(1)}, bf16[128,1024]{1,0:T(8,128)(2,1)}, u32[]{:S(2)}) copy-start(bf16[128,1024]{1,0:T(8,128)(2,1)} %param.9) | copy-start | bytes 786436
  29.8 125.1 %all-to-all-start = ((bf16[64,14,1024]{2,1,0:T(8,128)(2,1)}), bf16[64,14,1024]{2,1,0:T(8,128)(2,1)S(1)}, u32[]{:S(2)}, u32[]{:S(2)}) async-start(bf16[64,14,1024]{2,1,0:T(8,128)(2,1)} %pad_maximum_fusion), calls=%async_computation | async-start | bytes 4194304 | tf_op jit(solution)/shard_map/all_to_all | solution.py:14
  44.5 153.8 %reduce-scatter.3.cloned.1.call-start = ((), (), s32[]{:S(2)}) async-start(), calls=%async_computation.5 | async-start | bytes 1474560 | tf_op jit(solution)/shard_map/reduce_scatter | solution.py:33
  159.3 1.5 copy-start.4
  160.9 6.0 %copy-start.3 = (f32[448,1536]{1,0:T(8,128)S(1)}, f32[448,1536]{1,0:T(8,128)}, u32[]{:S(2)}) copy-start(f32[448,1536]{1,0:T(8,128)} %bitcast_convert_fusion) | copy-start | bytes 8257540
  164.4 0.9 copy-start.5
  164.4 1.3 copy-start.7
  171.3 1.3 copy-start.8
  172.7 2.4 %copy-start.6 = (bf16[448,768]{1,0:T(8,128)(2,1)S(1)}, bf16[448,768]{1,0:T(8,128)(2,1)}, u32[]{:S(2)}) copy-start(bf16[448,768]{1,0:T(8,128)(2,1)} %copy-done.5) | copy-start | bytes 2064388
  178.6 35.7 %all-to-all-start.1 = ((bf16[64,7,1024]{2,1,0:T(8,128)(2,1)}), bf16[64,7,1024]{2,1,0:T(8,128)(2,1)S(1)}, u32[]{:S(2)}, u32[]{:S(2)}) async-start(bf16[64,7,1024]{2,1,0:T(8,128)(2,1)} %reshape.168), calls=%async_computation.1 | async-start | bytes 2097152 | tf_op jit(solution)/shard_map/all_to_all | solution.py:130
  185.1 43.6 %reduce-scatter.5.cloned.1.call-start = ((), (), s32[]{:S(2)}) async-start(), calls=%async_computation.6 | async-start | bytes 442368 | tf_op jit(solution)/shard_map/reduce_scatter | solution.py:33
Sparse Core Ops, SparseCore 0:
  11.2 113.0 all-gather.1
  172.6 25.6 reduce-scatter.2
  201.0 27.6 reduce-scatter.4
where the time goes:
time: 238 us; the launch traced here: 237 us
  waiting for transfers between devices  145 us (61%)
  local copies, waits for them, and re-layouts  28.6 us (12%)
  starting transfers between devices  21.5 us (9%)
  matrix products  14.5 us (6%)
  between operations  14.1 us (6%)
  other arithmetic  13 us (5%)
    all_to_all x1, waiting for transfers between devices, side_by_side(): lax.all_to_all(both, axis, split_axis=split_dim, concat_axis=concat_dim,...  107 us
    reduce_scatter x2, waiting for transfers between devices, sum_in_order(): tiles = lax.psum_scatter(tiles, axes[k], scatter_dimension=0, tiled=True)  22.4 us
    all_to_all x1, waiting for transfers between devices, body(): lax.all_to_all(row_grad.astype(jnp.bfloat16).reshape(n_owner, cap, width)...  15.8 us
    all_to_all x1, starting transfers between devices, side_by_side(): lax.all_to_all(both, axis, split_axis=split_dim, concat_axis=concat_dim,...  14.7 us
    all_to_all x1, starting transfers between devices, body(): lax.all_to_all(row_grad.astype(jnp.bfloat16).reshape(n_owner, cap, width)...  6.49 us
  transfers between devices with their start and end apart: 5, of which 4 were waited for; matrix products, arithmetic and copies ran while one was open for 17% of the time, Pallas kernels for 0%

commit v1 on v0

v1 whole, which is shorter than its diff:
```python
import jax
import jax.numpy as jnp
from jax import lax
from jax.experimental import pallas as pl
from jax.experimental.pallas import tpu as pltpu
from jax.sharding import PartitionSpec as P

MESH = pl.DeviceIdType.MESH
F32 = jnp.float32
BF16 = jnp.bfloat16

N_X = 4
N_DP = 8
N_OWN = 64
CAP = 7
SLOTS = 448
TOK = 128
D = 1024
FF = 768
RANK = 256
LT = D // 128
PART = RANK // N_DP
BLK = 64
N_BLK = SLOTS // BLK


def iota(shape, dim):
    return lax.broadcasted_iota(jnp.int32, shape, dim)


def dot(a, b):
    return jnp.dot(a, b, preferred_element_type=F32)


def dot_t(a, b):
    return lax.dot_general(a, b, (((1,), (1,)), ((), ())), preferred_element_type=F32)


def t_dot(a, b):
    return lax.dot_general(a, b, (((0,), (0,)), ((), ())), preferred_element_type=F32)


def pack_rows(x, perm, buf, at):
    halves = []
    for h in range(2):
        part = x[32 * h : 32 * h + 32]
        halves.append(jnp.concatenate([part[:, 128 * j : 128 * j + 128] for j in range(LT)], axis=0))
    out = dot(perm, jnp.concatenate(halves, axis=1))
    for h in range(2):
        piece = out[:, 128 * h : 128 * h + 128].reshape(32, LT, 128).astype(BF16)
        buf[pl.ds(at + 32 * h, 32)] = piece


def unpack_rows(buf, at, perm_t):
    halves = [
        buf[pl.ds(at + 32 * h, 32)].astype(F32).reshape(32 * LT, 128).astype(BF16) for h in range(2)
    ]
    out = dot(perm_t, jnp.concatenate(halves, axis=1)).astype(BF16)
    rows = []
    for h in range(2):
        rows.append(
            jnp.concatenate(
                [out[32 * j : 32 * j + 32, 128 * h : 128 * h + 128] for j in range(LT)], axis=1
            )
        )
    return jnp.concatenate(rows, axis=0)


def wait_bytes(ref, sem):
    pltpu.make_async_copy(ref, ref, sem).wait()


def kernel(
    tok_ref, og_ref, ids_ref, probs_ref, pre_hbm, gate_ref, up_ref, down_ref, basis_ref,
    in_ref, proj_ref,
    pre_ref, full_d, full_g, full_u, full_b,
    pick_ref, wrow_ref, perm_ref, perm_t_ref,
    dy_send, dy_recv, x_send, x_recv, back_send, back_recv,
    dy_rows, x_rows, hg_ref, hid_ref, ug_ref, gg_ref, rows_ref,
    part_send, part_recv, cross_send, cross_recv,
    pre_sem, own_sem, w_send, y_sem, xa_sem, xb_sem,
    a_send, a_recv, a_own, r_send, r_recv,
):
    dp = lax.axis_index("dp")
    me = lax.axis_index("expert")
    hi, x = dp // N_X, lax.rem(dp, N_X)
    other = lax.rem(dp + N_X, N_DP)
    z, r = me // 8, lax.rem(me, 8)
    x_peers = [(hi * N_X + lax.rem(x + k, N_X), me) for k in (1, 3, 2)]
    partner = (other, me)

    def peer(k):
        return lax.rem(z + lax.rem(k, 8), 8) * 8 + lax.rem(r + k // 8, 8)

    barrier = pltpu.get_barrier_semaphore()
    for dev in x_peers + [partner]:
        pl.semaphore_signal(barrier, inc=1, device_id=dev, device_id_type=MESH)

    @pl.loop(1, N_OWN)
    def _(k):
        pl.semaphore_signal(barrier, inc=1, device_id=(dp, peer(k)), device_id_type=MESH)

    pre_copy = pltpu.make_async_copy(pre_hbm, pre_ref, pre_sem)
    pre_copy.start()
    pl.semaphore_wait(barrier, N_OWN + 3)

    mats = [(down_ref, full_d), (gate_ref, full_g), (up_ref, full_u), (basis_ref, full_b)]

    def remote(src, dst, send, recv, dev):
        pltpu.make_async_remote_copy(src, dst, send, recv, device_id=dev, device_id_type=MESH).start()

    for m, (own, full) in enumerate(mats):
        remote(own, full.at[dp], w_send.at[m], y_sem.at[m], partner)
    for m, (own, full) in enumerate(mats):
        for dev in x_peers:
            remote(own, full.at[dp], w_send.at[m], xa_sem.at[m], dev)
    for m, (own, full) in enumerate(mats):
        pltpu.make_async_copy(own, full.at[dp], own_sem.at[m]).start()

    o, i = iota((256, 256), 0), iota((256, 256), 1)
    perm_ref[...] = jnp.where(o == (i & 31) * 8 + (i >> 5), 1.0, 0.0).astype(BF16)
    perm_t_ref[...] = jnp.where(i == (o & 31) * 8 + (o >> 5), 1.0, 0.0).astype(BF16)
    experts = iota((N_OWN, TOK), 0)
    named = jnp.zeros((N_OWN, TOK), F32)
    weight = jnp.zeros((N_OWN, TOK), F32)
    for k in range(3):
        hit = jnp.broadcast_to(ids_ref[k : k + 1, :], (N_OWN, TOK)) == experts
        named = named + jnp.where(hit, 1.0, 0.0)
        weight = weight + jnp.where(hit, jnp.broadcast_to(probs_ref[k : k + 1, :], (N_OWN, TOK)), 0.0)
    earlier = jnp.where(iota((TOK, TOK), 0) < iota((TOK, TOK), 1), 1.0, 0.0).astype(BF16)
    before = dot(named.astype(BF16), earlier)
    rank = jnp.where(named > 0.0, before, -1.0).astype(BF16)
    rel = iota((SLOTS, N_OWN), 0) - CAP * iota((SLOTS, N_OWN), 1)
    spread = jnp.where((rel >= 0) & (rel < CAP), 1.0, 0.0)
    slot_rank = jnp.sum(spread * rel.astype(F32), axis=1, keepdims=True)
    at_rank = dot(spread.astype(BF16), rank)
    pick = jnp.where(at_rank == slot_rank, 1.0, 0.0)
    pick_ref[...] = pick.astype(BF16)
    weights = lax.dot_general(
        spread, weight, (((1,), (0,)), ((), ())),
        precision=lax.Precision.HIGHEST, preferred_element_type=F32,
    )
    wrow_ref[...] = jnp.broadcast_to(jnp.sum(pick * weights, axis=1, keepdims=True), (SLOTS, 128))

    def exchange(send, recv, n):
        @pl.loop(1, N_OWN)
        def _(k):
            d = peer(k)
            remote(
                send.at[pl.ds(d * CAP, CAP)], recv.at[pl.ds(me * CAP, CAP)],
                a_send.at[n], a_recv.at[n], (dp, d),
            )

        mine = pl.ds(me * CAP, CAP)
        pltpu.make_async_copy(send.at[mine], recv.at[mine], a_own.at[n]).start()

    def arrived(send, recv, n):
        mine = pl.ds(me * CAP, CAP)
        pltpu.make_async_copy(send.at[mine], recv.at[mine], a_own.at[n]).wait()
        wait_bytes(recv.at[pl.ds(0, SLOTS - CAP)], a_recv.at[n])

    @pl.loop(0, N_BLK)
    def _(b):
        at = pl.multiple_of(b * BLK, BLK)
        got = dot(pick_ref[pl.ds(at, BLK), :], og_ref[...])
        scale = wrow_ref[pl.ds(at, BLK), :]
        got = (got * jnp.concatenate([scale] * LT, axis=1)).astype(BF16)
        pack_rows(got, perm_ref[...], dy_send, at)

    exchange(dy_send, dy_recv, 0)

    @pl.loop(0, N_BLK)
    def _(b):
        at = pl.multiple_of(b * BLK, BLK)
        got = dot(pick_ref[pl.ds(at, BLK), :], tok_ref[...]).astype(BF16)
        pack_rows(got, perm_ref[...], x_send, at)

    for m, (own, full) in enumerate(mats):
        wait_bytes(full.at[0], y_sem.at[m])
        for dev in x_peers:
            remote(full.at[other], full.at[other], w_send.at[m], xb_sem.at[m], dev)

    exchange(x_send, x_recv, 1)

    def gathered(m):
        own, full = mats[m]
        pltpu.make_async_copy(own, full.at[dp], own_sem.at[m]).wait()
        wait_bytes(full.at[pl.ds(0, 3)], xa_sem.at[m])
        wait_bytes(full.at[pl.ds(0, 3)], xb_sem.at[m])

    arrived(dy_send, dy_recv, 0)

    @pl.loop(0, N_BLK)
    def _(b):
        at = pl.multiple_of(b * BLK, BLK)
        dy_rows[pl.ds(at, BLK), :] = unpack_rows(dy_recv, at, perm_t_ref[...])

    gathered(0)

    @pl.loop(0, FF // 256)
    def _(c):
        cols = pl.ds(pl.multiple_of(c * 256, 256), 256)
        hg_ref[:, cols] = dot(dy_rows[...], full_d[:, :, cols].reshape(D, 256))

    pre_copy.wait()

    @pl.loop(0, SLOTS // 16)
    def _(b):
        rows = pl.ds(pl.multiple_of(b * 16, 16), 16)
        g = pre_ref[rows, :FF].astype(F32)
        u = pre_ref[rows, FF:].astype(F32)
        h = hg_ref[rows, :]
        sig = jax.nn.sigmoid(g)
        gs = g * sig
        hid_ref[rows, :] = (gs * u).astype(BF16)
        ug_ref[rows, :] = (h * gs).astype(BF16)
        gg_ref[rows, :] = (h * u * sig * (1.0 + g * (1.0 - sig))).astype(BF16)

    gathered(1)
    gathered(2)

    @pl.loop(0, D // 256)
    def _(c):
        cols = pl.ds(pl.multiple_of(c * 256, 256), 256)
        two = pl.ds(c * 2, 2)
        total = dot_t(gg_ref[...], full_g[two].reshape(256, FF))
        total = total + dot_t(ug_ref[...], full_u[two].reshape(256, FF))
        rows_ref[:, cols] = total.astype(BF16)

    @pl.loop(0, N_BLK)
    def _(b):
        at = pl.multiple_of(b * BLK, BLK)
        pack_rows(rows_ref[pl.ds(at, BLK), :], perm_ref[...], back_send, at)

    exchange(back_send, back_recv, 2)

    gathered(3)
    basis = full_b[...].reshape(D, RANK)
    dy_proj = dot(dy_rows[...], basis).astype(BF16)

    def put(n, term):
        for q in range(N_DP):
            part_send[q % N_X, q // N_X, n] = term[PART * q : PART * (q + 1)].astype(BF16)

    put(2, t_dot(dy_proj, hid_ref[...]))
    arrived(x_send, x_recv, 1)

    @pl.loop(0, N_BLK)
    def _(b):
        at = pl.multiple_of(b * BLK, BLK)
        x_rows[pl.ds(at, BLK), :] = unpack_rows(x_recv, at, perm_t_ref[...])

    x_proj = dot(x_rows[...], basis).astype(BF16)
    put(0, t_dot(x_proj, gg_ref[...]))
    put(1, t_dot(x_proj, ug_ref[...]))

    for k, dev in enumerate(x_peers):
        to = lax.rem(x + (1, 3, 2)[k], N_X)
        remote(part_send.at[to], part_recv.at[k], r_send.at[0], r_recv.at[0], dev)
    wait_bytes(part_recv, r_recv.at[0])

    def sum_x(h):
        total = part_send[x, h].astype(F32)
        for k in range(3):
            total = total + part_recv[k, h].astype(F32)
        return total

    cross_send[...] = sum_x(1 - hi).astype(BF16)
    remote(cross_send, cross_recv, r_send.at[1], r_recv.at[1], partner)
    proj_ref[...] = sum_x(hi)

    arrived(back_send, back_recv, 2)

    @pl.loop(0, N_BLK)
    def _(b):
        at = pl.multiple_of(b * BLK, BLK)
        rows_ref[pl.ds(at, BLK), :] = unpack_rows(back_recv, at, perm_t_ref[...])

    in_ref[...] = t_dot(pick_ref[...], rows_ref[...]).astype(BF16)

    wait_bytes(cross_recv, r_recv.at[1])
    proj_ref[...] = proj_ref[...] + cross_recv[...].astype(F32)

    for m, (own, full) in enumerate(mats):
        wait_bytes(full.at[pl.ds(0, 7)], w_send.at[m])
    for n, buf in enumerate((dy_send, x_send, back_send)):
        wait_bytes(buf.at[pl.ds(0, SLOTS - CAP)], a_send.at[n])
    wait_bytes(part_recv, r_send.at[0])
    wait_bytes(cross_send, r_send.at[1])


def body(
    tokens, out_grad, expert_ids, gate_probs, saved_pre, gate_weight, up_weight, down_weight, basis
):
    vmem = pl.BlockSpec(memory_space=pltpu.VMEM)
    dma = pltpu.SemaphoreType.DMA
    packed = pltpu.VMEM((SLOTS, LT, 128), BF16)
    in_grad, proj = pl.pallas_call(
        kernel,
        out_shape=(
            jax.ShapeDtypeStruct((TOK, D), BF16),
            jax.ShapeDtypeStruct((3, PART, FF), F32),
        ),
        in_specs=[vmem] * 4 + [pl.BlockSpec(memory_space=pl.ANY)] + [vmem] * 4,
        out_specs=(vmem, vmem),
        scratch_shapes=[
            pltpu.VMEM((SLOTS, 2 * FF), BF16),
            pltpu.VMEM((N_DP, 128, FF), BF16),
            pltpu.VMEM((N_DP, 128, FF), BF16),
            pltpu.VMEM((N_DP, 128, FF), BF16),
            pltpu.VMEM((N_DP, 128, RANK), BF16),
            pltpu.VMEM((SLOTS, TOK), BF16),
            pltpu.VMEM((SLOTS, 128), F32),
            pltpu.VMEM((256, 256), BF16),
            pltpu.VMEM((256, 256), BF16),
            packed, packed, packed, packed, packed, packed,
            pltpu.VMEM((SLOTS, D), BF16),
            pltpu.VMEM((SLOTS, D), BF16),
            pltpu.VMEM((SLOTS, FF), F32),
            pltpu.VMEM((SLOTS, FF), BF16),
            pltpu.VMEM((SLOTS, FF), BF16),
            pltpu.VMEM((SLOTS, FF), BF16),
            pltpu.VMEM((SLOTS, D), BF16),
            pltpu.VMEM((N_X, 2, 3, PART, FF), BF16),
            pltpu.VMEM((3, 2, 3, PART, FF), BF16),
            pltpu.VMEM((3, PART, FF), BF16),
            pltpu.VMEM((3, PART, FF), BF16),
            dma, dma((4,)), dma((4,)), dma((4,)), dma((4,)), dma((4,)),
            dma((3,)), dma((3,)), dma((3,)), dma((2,)), dma((2,)),
        ],
        compiler_params=pltpu.CompilerParams(
            collective_id=0, has_side_effects=True, vmem_limit_bytes=48 << 20
        ),
    )(
        tokens, out_grad, expert_ids.T, gate_probs.T, saved_pre[0, 0],
        gate_weight[0], up_weight[0], down_weight[0], basis[0],
    )
    return in_grad, proj[None]


def solution(mesh):
    placed = (
        P(("dp", "expert"), None),
        P(("dp", "expert"), None),
        P(("dp", "expert"), None),
        P(("dp", "expert"), None),
        P("dp", "expert", None, None),
        P("expert", "dp", None),
        P("expert", "dp", None),
        P("expert", "dp", None),
        P("expert", "dp", None),
    )
    return jax.shard_map(
        body,
        mesh=mesh,
        in_specs=placed,
        out_specs=(P(("dp", "expert"), None), P("expert", None, "dp", None)),
        check_vma=False,
    )
```

time: 238 us -> 136 us (0.57)
  waiting for transfers between devices: 145 us -> 0 us
  Pallas kernels: 0 us -> 126 us
  starting transfers between devices: 21.5 us -> 0 us
  local copies, waits for them, and re-layouts: 28.6 us -> 9.63 us
  matrix products: 14.5 us -> 0 us
  between operations: 14.1 us -> 0.66 us
  other arithmetic: 13 us -> 0 us
    pallas_call x0 -> x1, Pallas kernels: none -> 126 us  [body(): pl.pallas_call(kernel, out_shape=(jax.ShapeDtypeStruct((TOK, D), BF16), j...]
    all_to_all x2 -> x0, waiting for transfers between devices: 123 us -> none  [the longest x1 107 us: side_by_side(): lax.all_to_all(both, axis, split_axis=split_dim, concat_axis=concat_dim,...]
    reduce_scatter x2 -> x0, waiting for transfers between devices: 22.4 us -> none  [sum_in_order(): tiles = lax.psum_scatter(tiles, axes[k], scatter_dimension=0, tiled=True)]
    all_to_all x2 -> x0, starting transfers between devices: 21.2 us -> none  [the longest x1 14.7 us: side_by_side(): lax.all_to_all(both, axis, split_axis=split_dim, concat_axis=concat_dim,...]
    dot_general x7 -> x0, matrix products: 14.5 us -> none  [the longest x3 4.72 us: contract_rows(): lax.dot_general(left, right, (((0,), (0,)), ((), ())), preferred_element_...]
    gather x6 -> x0, local copies, waits for them, and re-layouts: 11.7 us -> none  [the longest x1 4 us: body(): weight_pick = gate_probs[picked, fill_choice]]
    unnamed x20, local copies, waits for them, and re-layouts: 1.12 us -> 9.63 us
    reshape x8 -> x0, local copies, waits for them, and re-layouts: 6.07 us -> none  [the longest x1 1.45 us: body(): rows_in = arrived_rows.reshape(slots, width)]
  transfers between devices with their start and end apart: 5 -> 0, of which waited for: 4 -> 0; matrix products, arithmetic and copies ran while one was open for 17% -> 0% of each run, Pallas kernels for 0% -> 0%
where the time goes in v1:
time: 136 us
  Pallas kernels  126 us (93%)
  local copies, waits for them, and re-layouts  9.63 us (7%)
    pallas_call x1, Pallas kernels, body(): pl.pallas_call(kernel, out_shape=(jax.ShapeDtypeStruct((TOK, D), BF16), j...  126 us
    unnamed x20, local copies, waits for them, and re-layouts  9.63 us

profile of v1, /device:TPU:9, one launch (start us, length us, event | category | flops | bytes accessed | tf_op | source)
XLA Modules:
  0.0 135.9 jit_solution(6970718899533976487)
XLA Ops:
  0.6 0.0 copy-start
  0.6 1.3 copy-done
  2.0 0.0 copy-start.1
  2.0 0.9 copy-done.1
  2.9 0.0 copy-start.2
  2.9 0.9 copy-done.2
  3.9 0.0 copy-start.3
  3.9 0.9 copy-done.3
  4.8 0.0 copy-start.4
  4.8 0.9 copy-done.4
  5.7 0.0 copy-start.5
  5.7 0.9 copy-done.5
  6.7 0.0 copy-start.6
  6.7 0.8 copy-done.6
  7.5 0.0 copy-start.7
  7.5 0.7 copy-done.7
  8.2 0.0 copy-start.8
  8.2 0.7 copy-done.8
  8.9 125.6 %shard_map.104 = (bf16[128,1024]{1,0:T(8,128)(2,1)S(1)}, f32[3,32,768]{2,1,0:T(8,128)S(1)}) custom-call(bf16[128,1024]{1,0:T(8,128)(2,1)S(1)} %copy-done.1, bf16[128,1024]{1,0:T(8,128)(2,1)S(1)} %copy-done.2, s32[3,128]{1,0:T(4,128)S(1)} %bitcast.14, f32[3,128]{1,0:T(4,128)S(1)} %bitcast.15, bf16[448,1536]{1,0:T(8,128)(2,1)S(1)} %bitcast.8, ...), custom_call_target="tpu_custom_call" | custom-call | tf_op jit(solution)/shard_map/pallas_call | solution.py:298
  134.5 0.7 copy.13
  135.2 0.7 copy.14
Async XLA Ops:
  0.6 1.3 copy-start
  2.0 0.9 copy-start.1
  2.9 0.9 copy-start.2
  3.9 0.9 copy-start.3
  4.8 0.9 copy-start.4
  5.7 0.9 copy-start.5
  6.7 0.8 copy-start.6
  7.5 0.7 copy-start.7
  8.2 0.7 copy-start.8

commit v2 on v1

v2 whole, which is shorter than its diff:
```python
import jax
import jax.numpy as jnp
from jax import lax
from jax.experimental import pallas as pl
from jax.experimental.pallas import tpu as pltpu
from jax.sharding import PartitionSpec as P

MESH = pl.DeviceIdType.MESH
F32 = jnp.float32
BF16 = jnp.bfloat16

N_X = 4
N_DP = 8
N_OWN = 64
CAP = 7
SLOTS = 448
TOK = 128
D = 1024
FF = 768
RANK = 256
LT = D // 128
PART = RANK // N_DP
N_Y = 4
COL = SLOTS // N_Y


def iota(shape, dim):
    return lax.broadcasted_iota(jnp.int32, shape, dim)


def dot(a, b):
    return jnp.dot(a, b, preferred_element_type=F32)


def dot_t(a, b):
    return lax.dot_general(a, b, (((1,), (1,)), ((), ())), preferred_element_type=F32)


def t_dot(a, b):
    return lax.dot_general(a, b, (((0,), (0,)), ((), ())), preferred_element_type=F32)


def pack_rows(x, perm, buf, at):
    groups = []
    for g in range(COL // 16):
        part = x[16 * g : 16 * g + 16]
        groups.append(jnp.concatenate([part[:, 128 * j : 128 * j + 128] for j in range(LT)], axis=0))
    out = dot(perm, jnp.concatenate(groups, axis=1))
    for g in range(COL // 16):
        piece = out[:, 128 * g : 128 * g + 128].reshape(16, LT, 128).astype(BF16)
        buf[pl.ds(at + 16 * g, 16)] = piece


def unpack_rows(buf, at, perm_t):
    groups = [
        buf[pl.ds(at + 16 * g, 16)].astype(F32).reshape(16 * LT, 128).astype(BF16)
        for g in range(COL // 16)
    ]
    out = dot(perm_t, jnp.concatenate(groups, axis=1)).astype(BF16)
    rows = []
    for g in range(COL // 16):
        rows.append(
            jnp.concatenate(
                [out[16 * j : 16 * j + 16, 128 * g : 128 * g + 128] for j in range(LT)], axis=1
            )
        )
    return jnp.concatenate(rows, axis=0)


def wait_bytes(ref, sem):
    pltpu.make_async_copy(ref, ref, sem).wait()


def pick_slots(ids_ref, probs_ref, experts, earlier):
    n = experts.shape[0]
    named = jnp.zeros((n, TOK), F32)
    weight = jnp.zeros((n, TOK), F32)
    for k in range(3):
        hit = jnp.broadcast_to(ids_ref[k : k + 1, :], (n, TOK)) == experts
        named = named + jnp.where(hit, 1.0, 0.0)
        weight = weight + jnp.where(hit, jnp.broadcast_to(probs_ref[k : k + 1, :], (n, TOK)), 0.0)
    before = dot(named.astype(BF16), earlier)
    rank = jnp.where(named > 0.0, before, -1.0).astype(BF16)
    rel = iota((n * CAP, n), 0) - CAP * iota((n * CAP, n), 1)
    spread = jnp.where((rel >= 0) & (rel < CAP), 1.0, 0.0)
    slot_rank = jnp.sum(spread * rel.astype(F32), axis=1, keepdims=True)
    pick = jnp.where(dot(spread.astype(BF16), rank) == slot_rank, 1.0, 0.0)
    weights = lax.dot_general(
        spread, weight, (((1,), (0,)), ((), ())),
        precision=lax.Precision.HIGHEST, preferred_element_type=F32,
    )
    scale = jnp.broadcast_to(jnp.sum(pick * weights, axis=1, keepdims=True), (n * CAP, 128))
    return pick.astype(BF16), scale


def kernel(
    tok_hbm, og_hbm, ids_ref, probs_ref, pre_hbm, gate_hbm, up_hbm, down_hbm, basis_hbm,
    in_ref, proj_ref,
    tok_ref, og_ref, pre_ref, full_d, full_g, full_u, full_b,
    meta_ids, meta_probs, raw_ids, raw_probs, raw_tok, raw_og,
    pick_ref, col_pick, col_wrow, perm_ref, perm_t_ref,
    dy_send, dy_recv, x_send, x_recv, back_send, back_recv,
    dy_rows, x_rows, hg_ref, hid_ref, ug_ref, gg_ref, rows_ref,
    part_send, part_recv, cross_send, cross_recv,
    in_sem, own_sem, w_send, y_sem, x_sem,
    raw_send, raw_recv, a_send, a_recv, a_own, r_send, r_recv,
):
    dp = lax.axis_index("dp")
    me = lax.axis_index("expert")
    hi, x = dp // N_X, lax.rem(dp, N_X)
    other = lax.rem(dp + N_X, N_DP)
    z, r = me // 8, lax.rem(me, 8)
    core = lax.rem(r, 2)
    x_peers = [(hi * N_X + lax.rem(x + k, N_X), me) for k in (1, 3, 2)]
    right, left = x_peers[:2]
    partner = (other, me)

    def peer(k):
        return lax.rem(z + lax.rem(k, 8), 8), lax.rem(r + k // 8, 8)

    own_col = r // 2
    near_col = own_col + 1 - 2 * lax.rem(own_col, 2)
    far_cols = (lax.rem(own_col + 2, N_Y), lax.rem(near_col + 2, N_Y))
    cols = (own_col, near_col, *far_cols)
    near_dev = (dp, z * 8 + near_col * 2 + core)
    far_dev = (dp, z * 8 + far_cols[0] * 2 + core)

    def across(k):
        return lax.rem(z + lax.rem(3 * k + 4, 8), 8), lax.rem(lax.rem(r, 2) + k // 8, 2)

    def remote(src, dst, send, recv, dev):
        pltpu.make_async_remote_copy(src, dst, send, recv, device_id=dev, device_id_type=MESH).start()

    barrier = pltpu.get_barrier_semaphore()
    for dev in x_peers + [partner]:
        pl.semaphore_signal(barrier, inc=1, device_id=dev, device_id_type=MESH)

    @pl.loop(1, N_OWN)
    def _(k):
        to_z, to_r = peer(k)
        pl.semaphore_signal(barrier, inc=1, device_id=(dp, to_z * 8 + to_r), device_id_type=MESH)

    mats = [(down_hbm, full_d), (gate_hbm, full_g), (up_hbm, full_u), (basis_hbm, full_b)]
    own_copies = [pltpu.make_async_copy(own, full.at[dp], own_sem.at[m]) for m, (own, full) in enumerate(mats)]
    og_copy = pltpu.make_async_copy(og_hbm, og_ref, in_sem.at[0])
    tok_copy = pltpu.make_async_copy(tok_hbm, tok_ref, in_sem.at[1])
    pre_copy = pltpu.make_async_copy(pre_hbm, pre_ref, in_sem.at[2])
    for copy in [og_copy] + own_copies + [tok_copy, pre_copy]:
        copy.start()
    meta_ids[...] = jnp.zeros_like(meta_ids)
    meta_probs[...] = jnp.zeros_like(meta_probs)
    meta_ids[0:3, :] = ids_ref[...]
    meta_probs[0:3, :] = probs_ref[...]
    earlier = jnp.where(iota((TOK, TOK), 0) < iota((TOK, TOK), 1), 1.0, 0.0).astype(BF16)
    o, i = iota((128, 128), 0), iota((128, 128), 1)
    perm_ref[...] = jnp.where(o == (i & 15) * 8 + (i >> 4), 1.0, 0.0).astype(BF16)
    perm_t_ref[...] = jnp.where(i == (o & 15) * 8 + (o >> 4), 1.0, 0.0).astype(BF16)
    q = iota((N_OWN, TOK), 0)
    experts = ((q & 15) >> 1) * 8 + ((q >> 4) ^ own_col) * 2 + (q & 1)
    pick, scale = pick_slots(ids_ref, probs_ref, experts, earlier)
    pick_ref[...] = pick
    og_copy.wait()
    pl.semaphore_wait(barrier, N_OWN + 3)

    def cross_y(m):
        own, full = mats[m]
        remote(full.at[dp], full.at[dp], w_send.at[m], y_sem.at[m], partner)

    def to_sides(m, block, phase):
        full = mats[m][1]
        remote(full.at[block], full.at[block], w_send.at[m], x_sem.at[phase, 0, m], right)
        remote(full.at[block], full.at[block], w_send.at[m], x_sem.at[phase, 1, m], left)

    def pass_sides(m, phase):
        full = mats[m][1]
        row = (hi, 1 - hi)[phase] * N_X
        for side, frm, to in ((0, x + 3, right), (1, x + 1, left)):
            wait_bytes(full.at[0], x_sem.at[phase, side, m])
            piece = full.at[row + lax.rem(frm, N_X), pl.ds(64 * side, 64)]
            remote(piece, piece, w_send.at[m], x_sem.at[phase, 2, m], to)

    def pass_on(m):
        own, full = mats[m]
        wait_bytes(full.at[0], y_sem.at[m])
        to_sides(m, other, 1)

    def gathered(m):
        full = mats[m][1]
        wait_bytes(full.at[0], x_sem.at[0, 2, m])
        wait_bytes(full.at[0], x_sem.at[1, 2, m])

    def slots(index):
        return pl.ds(index * CAP, CAP)

    def send_slots(send, recv, n, j):
        slot = slots(z * 8 + cols[j] * 2 + core)

        @pl.loop(0, 16)
        def _(k):
            to_z, to_core = across(k)
            src, dst = send.at[slots(j * 16 + to_z * 2 + to_core)], recv.at[slot]

            @pl.when(k != 4)
            def _():
                remote(src, dst, a_send.at[n], a_recv.at[n], (dp, to_z * 8 + own_col * 2 + to_core))

        pltpu.make_async_copy(
            send.at[slots(j * 16 + z * 2 + core)], recv.at[slot], a_own.at[n]
        ).start()

    def arrived(recv, n, local):
        wait_bytes(recv.at[pl.ds(0, CAP * local)], a_own.at[n])
        wait_bytes(recv.at[pl.ds(0, SLOTS - CAP * local)], a_recv.at[n])

    def build(n, j, src, send):
        rows = pl.ds(j * COL, COL)
        got = dot(col_pick[rows, :], src[...])
        if n == 0:
            got = got * jnp.concatenate([col_wrow[rows, :]] * LT, axis=1)
        pack_rows(got.astype(BF16), perm_ref[...], send, j * COL)

    raws = (meta_ids, meta_probs, og_ref, tok_ref)
    others = (raw_ids, raw_probs, raw_og, raw_tok)

    def send_raw(n):
        remote(raws[n], others[n].at[1], raw_send.at[n], raw_recv.at[n, 1], far_dev)
        remote(raws[n], others[n].at[0], raw_send.at[n], raw_recv.at[n, 0], near_dev)

    def take_raw(n, j):
        wait_bytes(others[n].at[0], raw_recv.at[n, j - 1])
        if j == 2:
            remote(others[n].at[1], others[n].at[2], raw_send.at[n], raw_recv.at[n, 2], near_dev)

    def take_meta(j):
        take_raw(0, j)
        take_raw(1, j)
        pick, scale = pick_slots(raw_ids.at[j - 1], raw_probs.at[j - 1], experts[:16], earlier)
        col_pick[COL * j : COL * (j + 1)] = pick
        col_wrow[COL * j : COL * (j + 1)] = scale

    def deliver(n, j):
        src, send, recv = ((og_ref, dy_send, dy_recv), (tok_ref, x_send, x_recv))[n]
        if j:
            if n == 0:
                take_meta(j)
                take_raw(2, j)
            elif j != 2:
                take_raw(3, j)
            src = others[n + 2].at[j - 1]
        build(n, j, src, send)
        send_slots(send, recv, n, j)

    for n in range(3):
        send_raw(n)
    for copy in own_copies:
        copy.wait()
    for m in range(3):
        to_sides(m, dp, 0)
    cross_y(0)
    col_pick[0:COL] = pick_ref[0:COL]
    col_wrow[0:COL] = scale[0:COL]
    deliver(0, 0)
    pass_sides(0, 0)
    deliver(0, 1)
    deliver(0, 2)
    cross_y(1)
    tok_copy.wait()
    send_raw(3)
    pass_sides(1, 0)
    pass_sides(2, 0)
    pass_on(0)
    deliver(0, 3)
    deliver(1, 0)
    pass_sides(0, 1)
    pass_on(1)
    cross_y(2)
    cross_y(3)
    to_sides(3, dp, 0)
    take_raw(3, 2)
    arrived(dy_recv, 0, 4)

    @pl.loop(0, N_Y)
    def _(b):
        at = pl.multiple_of(b * COL, 16)
        dy_rows[pl.ds(at, COL), :] = unpack_rows(dy_recv, at, perm_t_ref[...])

    deliver(1, 1)
    deliver(1, 2)
    gathered(0)

    @pl.loop(0, FF // 256)
    def _(c):
        cols = pl.ds(pl.multiple_of(c * 256, 256), 256)
        hg_ref[:, cols] = dot(dy_rows[...], full_d[:, :, cols].reshape(D, 256))

    pass_sides(1, 1)
    pass_sides(3, 0)
    pre_copy.wait()

    @pl.loop(0, SLOTS // 16)
    def _(b):
        rows = pl.ds(pl.multiple_of(b * 16, 16), 16)
        g = pre_ref[rows, :FF].astype(F32)
        u = pre_ref[rows, FF:].astype(F32)
        h = hg_ref[rows, :]
        sig = jax.nn.sigmoid(g)
        gs = g * sig
        hid_ref[rows, :] = (gs * u).astype(BF16)
        ug_ref[rows, :] = (h * gs).astype(BF16)
        gg_ref[rows, :] = (h * u * sig * (1.0 + g * (1.0 - sig))).astype(BF16)

    pass_on(2)
    pass_on(3)
    deliver(1, 3)
    pass_sides(2, 1)
    pass_sides(3, 1)
    gathered(1)
    gathered(2)

    @pl.loop(0, D // 256)
    def _(c):
        cols = pl.ds(pl.multiple_of(c * 256, 256), 256)
        two = pl.ds(c * 2, 2)
        total = dot_t(gg_ref[...], full_g[two].reshape(256, FF))
        total = total + dot_t(ug_ref[...], full_u[two].reshape(256, FF))
        rows_ref[:, cols] = total.astype(BF16)

    @pl.loop(0, N_Y)
    def _(b):
        at = pl.multiple_of(b * COL, 16)
        pack_rows(rows_ref[pl.ds(at, COL), :], perm_ref[...], back_send, at)

    def place(to_r):
        col = to_r // 2
        apart = 2 * lax.rem(col // 2 + own_col // 2, 2) + lax.rem(col + own_col, 2)
        return slots(apart * 16 + z * 2 + core)

    def give_back(to_z, to_r):
        remote(
            back_send.at[slots(to_z * 8 + to_r)], back_recv.at[place(to_r)],
            a_send.at[2], a_recv.at[2], (dp, to_z * 8 + to_r),
        )

    @pl.loop(0, 16)
    def _(k):
        to_z, to_core = across(k)
        for col in (*far_cols, near_col):
            give_back(to_z, col * 2 + to_core)

        @pl.when(k != 4)
        def _():
            give_back(to_z, own_col * 2 + to_core)

    pltpu.make_async_copy(back_send.at[slots(me)], back_recv.at[place(r)], a_own.at[2]).start()

    gathered(3)
    basis = full_b[...].reshape(D, RANK)
    dy_proj = dot(dy_rows[...], basis).astype(BF16)

    def put(n, term):
        for p in range(N_DP):
            part_send[p % N_X, p // N_X, n] = term[PART * p : PART * (p + 1)].astype(BF16)

    put(2, t_dot(dy_proj, hid_ref[...]))
    arrived(x_recv, 1, 4)

    @pl.loop(0, N_Y)
    def _(b):
        at = pl.multiple_of(b * COL, 16)
        x_rows[pl.ds(at, COL), :] = unpack_rows(x_recv, at, perm_t_ref[...])

    x_proj = dot(x_rows[...], basis).astype(BF16)
    put(0, t_dot(x_proj, gg_ref[...]))
    put(1, t_dot(x_proj, ug_ref[...]))

    for k, dev in enumerate(x_peers):
        to = lax.rem(x + (1, 3, 2)[k], N_X)
        remote(part_send.at[to], part_recv.at[k], r_send.at[0], r_recv.at[0], dev)

    wait_bytes(part_recv, r_recv.at[0])

    def sum_x(h):
        total = part_send[x, h].astype(F32)
        for k in range(3):
            total = total + part_recv[k, h].astype(F32)
        return total

    cross_send[...] = sum_x(1 - hi).astype(BF16)
    remote(cross_send, cross_recv, r_send.at[1], r_recv.at[1], partner)
    proj_ref[...] = sum_x(hi)

    arrived(back_recv, 2, 1)

    @pl.loop(0, N_Y)
    def _(b):
        at = pl.multiple_of(b * COL, 16)
        rows_ref[pl.ds(at, COL), :] = unpack_rows(back_recv, at, perm_t_ref[...])

    in_ref[...] = t_dot(pick_ref[...], rows_ref[...]).astype(BF16)

    wait_bytes(cross_recv, r_recv.at[1])
    proj_ref[...] = proj_ref[...] + cross_recv[...].astype(F32)

    for m, (own, full) in enumerate(mats):
        wait_bytes(full.at[pl.ds(0, 7)], w_send.at[m])
    for n, dst in enumerate(others):
        wait_bytes(dst, raw_send.at[n])
    for n, buf, local in ((0, dy_send, 4), (1, x_send, 4), (2, back_send, 1)):
        wait_bytes(buf.at[pl.ds(0, SLOTS - CAP * local)], a_send.at[n])
    wait_bytes(part_recv, r_send.at[0])
    wait_bytes(cross_send, r_send.at[1])


def body(
    tokens, out_grad, expert_ids, gate_probs, saved_pre, gate_weight, up_weight, down_weight, basis
):
    vmem = pl.BlockSpec(memory_space=pltpu.VMEM)
    anywhere = pl.BlockSpec(memory_space=pl.ANY)
    dma = pltpu.SemaphoreType.DMA
    packed = pltpu.VMEM((SLOTS, LT, 128), BF16)
    in_grad, proj = pl.pallas_call(
        kernel,
        out_shape=(
            jax.ShapeDtypeStruct((TOK, D), BF16),
            jax.ShapeDtypeStruct((3, PART, FF), F32),
        ),
        in_specs=[anywhere] * 2 + [vmem] * 2 + [anywhere] * 5,
        out_specs=(vmem, vmem),
        scratch_shapes=[
            pltpu.VMEM((TOK, D), BF16),
            pltpu.VMEM((TOK, D), BF16),
            pltpu.VMEM((SLOTS, 2 * FF), BF16),
            pltpu.VMEM((N_DP, 128, FF), BF16),
            pltpu.VMEM((N_DP, 128, FF), BF16),
            pltpu.VMEM((N_DP, 128, FF), BF16),
            pltpu.VMEM((N_DP, 128, RANK), BF16),
            pltpu.VMEM((8, TOK), jnp.int32),
            pltpu.VMEM((8, TOK), F32),
            pltpu.VMEM((3, 8, TOK), jnp.int32),
            pltpu.VMEM((3, 8, TOK), F32),
            pltpu.VMEM((3, TOK, D), BF16),
            pltpu.VMEM((3, TOK, D), BF16),
            pltpu.VMEM((SLOTS, TOK), BF16),
            pltpu.VMEM((SLOTS, TOK), BF16),
            pltpu.VMEM((SLOTS, 128), F32),
            pltpu.VMEM((128, 128), BF16),
            pltpu.VMEM((128, 128), BF16),
            packed, packed, packed, packed, packed, packed,
            pltpu.VMEM((SLOTS, D), BF16),
            pltpu.VMEM((SLOTS, D), BF16),
            pltpu.VMEM((SLOTS, FF), F32),
            pltpu.VMEM((SLOTS, FF), BF16),
            pltpu.VMEM((SLOTS, FF), BF16),
            pltpu.VMEM((SLOTS, FF), BF16),
            pltpu.VMEM((SLOTS, D), BF16),
            pltpu.VMEM((N_X, 2, 3, PART, FF), BF16),
            pltpu.VMEM((3, 2, 3, PART, FF), BF16),
            pltpu.VMEM((3, PART, FF), BF16),
            pltpu.VMEM((3, PART, FF), BF16),
            dma((3,)), dma((4,)), dma((4,)), dma((4,)), dma((2, 3, 4)),
            dma((4,)), dma((4, 3)), dma((3,)), dma((3,)), dma((3,)), dma((2,)), dma((2,)),
        ],
        compiler_params=pltpu.CompilerParams(
            collective_id=0, has_side_effects=True, vmem_limit_bytes=67043328
        ),
    )(
        tokens, out_grad, expert_ids.T, gate_probs.T, saved_pre[0, 0],
        gate_weight[0], up_weight[0], down_weight[0], basis[0],
    )
    return in_grad, proj[None]


def solution(mesh):
    placed = (
        P(("dp", "expert"), None),
        P(("dp", "expert"), None),
        P(("dp", "expert"), None),
        P(("dp", "expert"), None),
        P("dp", "expert", None, None),
        P("expert", "dp", None),
        P("expert", "dp", None),
        P("expert", "dp", None),
        P("expert", "dp", None),
    )
    return jax.shard_map(
        body,
        mesh=mesh,
        in_specs=placed,
        out_specs=(P(("dp", "expert"), None), P("expert", None, "dp", None)),
        check_vma=False,
    )
```

time: 136 us -> 123 us (0.904)
  the two profiles are of different devices: /device:TPU:9 before, /device:TPU:3 now
where the time goes in v2:
time: 123 us; the launch traced here: 122 us
  Pallas kernels  118 us (96%)
  local copies, waits for them, and re-layouts  3.36 us (3%)
    pallas_call x1, Pallas kernels, body(): pl.pallas_call(kernel, out_shape=(jax.ShapeDtypeStruct((TOK, D), BF16), j...  118 us
    unnamed x2, local copies, waits for them, and re-layouts  3.36 us

profile of v2, /device:TPU:3, one launch (start us, length us, event | category | flops | bytes accessed | tf_op | source)
XLA Modules:
  0.0 122.3 jit_solution(9744224236243161205)
XLA Ops:
  0.6 118.3 %shard_map.104 = (bf16[128,1024]{1,0:T(8,128)(2,1)}, f32[3,32,768]{2,1,0:T(8,128)}) custom-call(bf16[128,1024]{1,0:T(8,128)(2,1)} %tok_hbm.1, bf16[128,1024]{1,0:T(8,128)(2,1)} %og_hbm.1, s32[3,128]{1,0:T(4,128)} %bitcast.14, f32[3,128]{1,0:T(4,128)} %bitcast.15, bf16[448,1536]{1,0:T(8,128)(2,1)} %bitcast.8, bf16[128,768]{1,0:T(8,128)(2,1)} %bitcast.10, ...), custom_call_target="tpu_custom_call" | custom-call | tf_op jit(solution)/shard_map/pallas_call | solution.py:421
  119.0 1.7 %copy.13 = bf16[128,1024]{1,0:T(8,128)(2,1)} copy(bf16[128,1024]{1,0:T(8,128)(2,1)} %get-tuple-element.8) | data formatting | bytes 524288
  120.6 1.7 %copy.14 = f32[1,3,32,768]{3,2,1,0:T(8,128)} copy(f32[1,3,32,768]{3,2,1,0:T(8,128)} %bitcast.9) | data formatting | bytes 589824

commit v3 on v2

--- a/solution.py
+++ b/solution.py
@@ -268,14 +268,14 @@
     send_raw(3)
     pass_sides(1, 0)
     pass_sides(2, 0)
-    pass_on(0)
     deliver(0, 3)
     deliver(1, 0)
+    pass_on(0)
     pass_sides(0, 1)
-    pass_on(1)
     cross_y(2)
     cross_y(3)
     to_sides(3, dp, 0)
+    pass_on(1)
     take_raw(3, 2)
     arrived(dy_recv, 0, 4)
 
@@ -409,6 +409,21 @@
         wait_bytes(buf.at[pl.ds(0, SLOTS - CAP * local)], a_send.at[n])
     wait_bytes(part_recv, r_send.at[0])
     wait_bytes(cross_send, r_send.at[1])
+
+
+def hand_out(a_hbm, b_hbm, a_out, b_out, a_ref, b_ref, sem):
+    a_in = pltpu.make_async_copy(a_hbm, a_ref, sem.at[0])
+    b_in = pltpu.make_async_copy(b_hbm, b_ref, sem.at[1])
+    a_in.start()
+    b_in.start()
+    a_in.wait()
+    a_back = pltpu.make_async_copy(a_ref, a_out, sem.at[2])
+    a_back.start()
+    b_in.wait()
+    b_back = pltpu.make_async_copy(b_ref, b_out, sem.at[3])
+    b_back.start()
+    a_back.wait()
+    b_back.wait()
 
 
 def body(
@@ -467,6 +482,17 @@
         tokens, out_grad, expert_ids.T, gate_probs.T, saved_pre[0, 0],
         gate_weight[0], up_weight[0], down_weight[0], basis[0],
     )
+    in_grad, proj = pl.pallas_call(
+        hand_out,
+        out_shape=(
+            jax.ShapeDtypeStruct((TOK, D), BF16),
+            jax.ShapeDtypeStruct((3, PART, FF), F32),
+        ),
+        in_specs=[anywhere, anywhere],
+        out_specs=(anywhere, anywhere),
+        scratch_shapes=[pltpu.VMEM((TOK, D), BF16), pltpu.VMEM((3, PART, FF), F32), dma((4,))],
+        compiler_params=pltpu.CompilerParams(vmem_limit_bytes=67043328),
+    )(in_grad, proj)
     return in_grad, proj[None]
 
 

time: 123 us -> 121 us (0.984)
  the two profiles are of different devices: /device:TPU:3 before, /device:TPU:41 now
where the time goes in v3:
time: 121 us
  Pallas kernels  120 us (99%)
    pallas_call x1, Pallas kernels, body(): pl.pallas_call(kernel, out_shape=(jax.ShapeDtypeStruct((TOK, D), BF16), j...  118 us

profile of v3, /device:TPU:41, one launch (start us, length us, event | category | flops | bytes accessed | tf_op | source)
XLA Modules:
  0.0 120.5 jit_solution(15285003160038671572)
XLA Ops:
  0.6 118.1 %shard_map.104 = (bf16[128,1024]{1,0:T(8,128)(2,1)}, f32[3,32,768]{2,1,0:T(8,128)}) custom-call(bf16[128,1024]{1,0:T(8,128)(2,1)} %tok_hbm.1, bf16[128,1024]{1,0:T(8,128)(2,1)} %og_hbm.1, s32[3,128]{1,0:T(4,128)} %bitcast.13, f32[3,128]{1,0:T(4,128)} %bitcast.14, bf16[448,1536]{1,0:T(8,128)(2,1)} %bitcast.8, bf16[128,768]{1,0:T(8,128)(2,1)} %bitcast.9, ...), custom_call_target="tpu_custom_call" | custom-call | tf_op jit(solution)/shard_map/pallas_call | solution.py:436
  118.7 1.8 %shard_map.105 = (bf16[128,1024]{1,0:T(8,128)(2,1)}, f32[3,32,768]{2,1,0:T(8,128)}) custom-call(bf16[128,1024]{1,0:T(8,128)(2,1)} %get-tuple-element.6.a_hbm, f32[3,32,768]{2,1,0:T(8,128)} %get-tuple-element.7.b_hbm), custom_call_target="tpu_custom_call" | custom-call | tf_op jit(solution)/shard_map/pallas_call | solution.py:485
